TPU v7x, 32 devices: a whole 2x2x4 slice. The times are simulated.
32 devices in a mesh: rows: 16 (over z, x, core), cols: 2 (over y).
Axes of the slice: x: 2, y: 2, z: 4, core: 2. Of those that a mesh axis runs over, the one named last changes fastest.
Arguments:
- rhs: float32 [8192, 16], P(('rows', 'cols')), may hold values from -6 to 6
- diagonal: float32 [8192], P(('rows', 'cols')), may hold values from 1 to 16
- blocks: float32 [64, 4, 128, 128], P('rows', 'cols'), may hold values from -0.15625 to 0.15625
- block_cols: int32 [64, 4], P('rows', 'cols'), may hold values from 0 to 31
- counts: int32 [64, 2], P('rows', 'cols'), may hold values from 1 to 2
Outputs:
- solution: float32 [8192, 16], P(('rows', 'cols'))
Inputs may be any that keep to these rules, and one draw needn't show every extreme that they name: Every entry of block_cols names a block column within its slot's group, from 0 to 31; entries may repeat within a row. `counts`: every count lies between 1 and 2; the slots past the count in a group hold blocks that are not used.
All inputs are finite; a program needn't handle non-finite values.
Results may differ from a plain program's by a relative error of at most 0.0001.
Values sent between devices are 32-bit elements; how exact they have to be, the bound alone decides.
A program may use at most 64 MiB of HBM per device.

v0:
```python
import jax
import jax.numpy as jnp
from jax import lax
from jax.sharding import PartitionSpec as P

ITERS = 4


def solve_block(matrix, right):
    size = matrix.shape[0]
    joined = jnp.concatenate([matrix, right], axis=1)
    for index in range(size):
        pivot_row = joined[index] / joined[index, index]
        joined = joined - joined[:, index : index + 1] * pivot_row[None, :]
        joined = joined.at[index].set(pivot_row)
    return joined[:, size:]


def gram(left, right):
    return jnp.dot(left.T, right, precision=lax.Precision.HIGHEST)


def times_block(vectors, small):
    return jnp.dot(vectors, small, precision=lax.Precision.HIGHEST)


def per_device(rhs, diagonal, blocks, block_cols, counts):
    width = blocks.shape[2]
    piece_rows = rhs.shape[0]
    used = (lax.broadcasted_iota(jnp.int32, block_cols.shape, 1) < counts).astype(jnp.float32)

    def block_rows(gathered, count):
        number = count // width
        segment = gathered.reshape(-1, width, gathered.shape[1])
        picked = segment[block_cols] * used[:, :, None, None]
        product = jnp.einsum("rkij,rkjs->ris", blocks, picked, precision=lax.Precision.HIGHEST)
        return product.reshape(number * width, gathered.shape[1])

    def product_of(piece):
        gathered = lax.all_gather(piece, "rows", axis=0, tiled=True)
        total = block_rows(gathered, blocks.shape[0] * width)
        return lax.psum(total, "cols")

    start_rows, diag_rows = (
        lax.all_gather(rhs, "cols", axis=0, tiled=True),
        lax.all_gather(diagonal, "cols", axis=0, tiled=True),
    )
    offset = lax.axis_index("cols") * piece_rows

    def apply(vectors):
        piece = lax.dynamic_slice_in_dim(vectors, offset, piece_rows, 0)
        return diag_rows[:, None] * vectors + product_of(piece)

    solution = jnp.zeros_like(start_rows)
    residual = start_rows
    direction = start_rows
    for iteration in range(ITERS):
        image = apply(direction)
        matrix, right = lax.psum((gram(start_rows, image), gram(start_rows, residual)), "rows")
        alpha = solve_block(matrix, right)
        middle = residual - times_block(image, alpha)
        second = apply(middle)
        along, square, cross = lax.psum(
            (jnp.sum(second * middle), jnp.sum(second * second), gram(start_rows, second)), "rows"
        )
        omega = along / square
        solution = solution + times_block(direction, alpha) + omega * middle
        residual = middle - omega * second
        beta = -solve_block(matrix, cross)
        direction = residual + times_block(direction - omega * image, beta)
    return lax.dynamic_slice_in_dim(solution, offset, piece_rows, 0)


def solution(mesh):
    in_specs = (
        P(("rows", "cols"), None),
        P(("rows", "cols")),
        P("rows", "cols", None, None),
        P("rows", "cols"),
        P("rows", "cols"),
    )
    out_specs = P(("rows", "cols"), None)
    return jax.shard_map(
        per_device, mesh=mesh, in_specs=in_specs, out_specs=out_specs, check_vma=False
    )
```

profile of v0, /device:TPU:0, one launch (start us, length us, event | category | flops | bytes accessed | tf_op | source)
XLA Modules:
  0.0 784.2 jit_solution(16636919881158414598)
XLA Ops:
  2.2 5.2 all-gather
  7.4 4.4 all_gather.31
  11.9 22.9 %all_gather.32 = f32[4096,16]{0,1:T(8,128)S(1)} all-gather(f32[256,16]{0,1:T(8,128)S(1)} %constant_dynamic-slice_fusion.7), channel_id=1, replica_groups=mesh['rows'=16,'cols'=2] {'rows'}, dimensions={0}, use_global_device_ids=true | all-gather | bytes 278528 | tf_op jit(solution)/shard_map/all_gather | solution.py:40
  36.0 8.4 %psum.189 = f32[512,16]{0,1:T(8,128)S(1)} all-reduce(f32[512,16]{0,1:T(8,128)S(1)} %bitcast.530), channel_id=1, replica_groups=mesh['rows'=16,'cols'=2] {'cols'}, use_global_device_ids=true, to_apply=%region_0.0 | all-reduce | flops 8192 | bytes 65536 | tf_op jit(solution)/shard_map/psum | solution.py:42
  44.5 57.6 %all-reduce.7 = (f32[16,16]{0,1:T(8,128)S(1)}, f32[16,16]{0,1:T(8,128)S(1)}) all-reduce(f32[16,16]{0,1:T(8,128)S(1)} %convolution_bitcast_fusion.18, f32[16,16]{0,1:T(8,128)S(1)} %fusion.156), channel_id=1, replica_groups=mesh['rows'=16,'cols'=2] {'rows'}, use_global_device_ids=true, to_apply=%region_1.0 | all-reduce | flops 512 | bytes 4096 | tf_op jit(solution)/shard_map/psum | solution.py:59
  106.0 0.9 fusion.153
  120.0 0.9 fusion.145
  130.1 17.8 %all_gather.33 = f32[4096,16]{0,1:T(8,128)S(1)} all-gather(f32[256,16]{0,1:T(8,128)S(1)} %constant_dynamic-slice_fusion.6), channel_id=1, replica_groups=mesh['rows'=16,'cols'=2] {'rows'}, dimensions={0}, use_global_device_ids=true | all-gather | bytes 278528 | tf_op jit(solution)/shard_map/all_gather | solution.py:40
  149.1 7.4 psum.192
  157.3 31.1 %all-reduce.6 = (f32[]{:T(128)}, f32[]{:T(128)}, f32[16,16]{0,1:T(8,128)S(1)}) all-reduce(f32[]{:T(128)} %get-tuple-element.1356, f32[]{:T(128)} %get-tuple-element.1355, f32[16,16]{0,1:T(8,128)S(1)} %convolution_bitcast_fusion.17), channel_id=1, replica_groups=mesh['rows'=16,'cols'=2] {'rows'}, use_global_device_ids=true, to_apply=%region_5.0 | all-reduce | flops 258 | bytes 2064 | tf_op jit(solution)/shard_map/psum | solution.py:63
  215.6 17.9 %all_gather.34 = f32[4096,16]{0,1:T(8,128)S(1)} all-gather(f32[256,16]{0,1:T(8,128)S(1)} %constant_dynamic-slice_fusion.5), channel_id=1, replica_groups=mesh['rows'=16,'cols'=2] {'rows'}, dimensions={0}, use_global_device_ids=true | all-gather | bytes 278528 | tf_op jit(solution)/shard_map/all_gather | solution.py:40
  234.7 8.4 %psum.196 = f32[512,16]{0,1:T(8,128)S(1)} all-reduce(f32[512,16]{0,1:T(8,128)S(1)} %bitcast.532), channel_id=1, replica_groups=mesh['rows'=16,'cols'=2] {'cols'}, use_global_device_ids=true, to_apply=%region_9.0 | all-reduce | flops 8192 | bytes 65536 | tf_op jit(solution)/shard_map/psum | solution.py:42
  243.3 57.6 %all-reduce.5 = (f32[16,16]{0,1:T(8,128)S(1)}, f32[16,16]{0,1:T(8,128)S(1)}) all-reduce(f32[16,16]{0,1:T(8,128)S(1)} %convolution_bitcast_fusion.16, f32[16,16]{0,1:T(8,128)S(1)} %convolution_bitcast_fusion.15), channel_id=1, replica_groups=mesh['rows'=16,'cols'=2] {'rows'}, use_global_device_ids=true, to_apply=%region_10.0 | all-reduce | flops 512 | bytes 4096 | tf_op jit(solution)/shard_map/psum | solution.py:59
  303.0 0.9 fusion.122
  306.5 0.9 fusion.120
  313.7 0.9 fusion.116
  317.2 0.9 fusion.114
  329.2 17.8 %all_gather.35 = f32[4096,16]{0,1:T(8,128)S(1)} all-gather(f32[256,16]{0,1:T(8,128)S(1)} %constant_dynamic-slice_fusion.4), channel_id=1, replica_groups=mesh['rows'=16,'cols'=2] {'rows'}, dimensions={0}, use_global_device_ids=true | all-gather | bytes 278528 | tf_op jit(solution)/shard_map/all_gather | solution.py:40
  348.2 7.4 psum.199
  356.4 31.1 %all-reduce.4 = (f32[]{:T(128)}, f32[]{:T(128)}, f32[16,16]{0,1:T(8,128)S(1)}) all-reduce(f32[]{:T(128)} %get-tuple-element.1354, f32[]{:T(128)} %get-tuple-element.1353, f32[16,16]{0,1:T(8,128)S(1)} %convolution_bitcast_fusion.14), channel_id=1, replica_groups=mesh['rows'=16,'cols'=2] {'rows'}, use_global_device_ids=true, to_apply=%region_14.0 | all-reduce | flops 258 | bytes 2064 | tf_op jit(solution)/shard_map/psum | solution.py:63
  414.6 17.9 %all_gather.36 = f32[4096,16]{0,1:T(8,128)S(1)} all-gather(f32[256,16]{0,1:T(8,128)S(1)} %constant_dynamic-slice_fusion.3), channel_id=1, replica_groups=mesh['rows'=16,'cols'=2] {'rows'}, dimensions={0}, use_global_device_ids=true | all-gather | bytes 278528 | tf_op jit(solution)/shard_map/all_gather | solution.py:40
  433.7 8.4 %psum.203 = f32[512,16]{0,1:T(8,128)S(1)} all-reduce(f32[512,16]{0,1:T(8,128)S(1)} %bitcast.534), channel_id=1, replica_groups=mesh['rows'=16,'cols'=2] {'cols'}, use_global_device_ids=true, to_apply=%region_18.0 | all-reduce | flops 8192 | bytes 65536 | tf_op jit(solution)/shard_map/psum | solution.py:42
  442.2 57.6 %all-reduce.3 = (f32[16,16]{0,1:T(8,128)S(1)}, f32[16,16]{0,1:T(8,128)S(1)}) all-reduce(f32[16,16]{0,1:T(8,128)S(1)} %convolution_bitcast_fusion.13, f32[16,16]{0,1:T(8,128)S(1)} %convolution_bitcast_fusion.12), channel_id=1, replica_groups=mesh['rows'=16,'cols'=2] {'rows'}, use_global_device_ids=true, to_apply=%region_19.0 | all-reduce | flops 512 | bytes 4096 | tf_op jit(solution)/shard_map/psum | solution.py:59
  528.2 17.8 %all_gather.37 = f32[4096,16]{0,1:T(8,128)S(1)} all-gather(f32[256,16]{0,1:T(8,128)S(1)} %constant_dynamic-slice_fusion.2), channel_id=1, replica_groups=mesh['rows'=16,'cols'=2] {'rows'}, dimensions={0}, use_global_device_ids=true | all-gather | bytes 278528 | tf_op jit(solution)/shard_map/all_gather | solution.py:40
  547.2 7.4 psum.206
  555.4 31.1 %all-reduce.2 = (f32[]{:T(128)}, f32[]{:T(128)}, f32[16,16]{0,1:T(8,128)S(1)}) all-reduce(f32[]{:T(128)} %get-tuple-element.1352, f32[]{:T(128)} %get-tuple-element.1351, f32[16,16]{0,1:T(8,128)S(1)} %convolution_bitcast_fusion.11), channel_id=1, replica_groups=mesh['rows'=16,'cols'=2] {'rows'}, use_global_device_ids=true, to_apply=%region_23.0 | all-reduce | flops 258 | bytes 2064 | tf_op jit(solution)/shard_map/psum | solution.py:63
  613.6 17.9 %all_gather.38 = f32[4096,16]{0,1:T(8,128)S(1)} all-gather(f32[256,16]{0,1:T(8,128)S(1)} %constant_dynamic-slice_fusion.1), channel_id=1, replica_groups=mesh['rows'=16,'cols'=2] {'rows'}, dimensions={0}, use_global_device_ids=true | all-gather | bytes 278528 | tf_op jit(solution)/shard_map/all_gather | solution.py:40
  632.7 8.4 %psum.210 = f32[512,16]{0,1:T(8,128)S(1)} all-reduce(f32[512,16]{0,1:T(8,128)S(1)} %bitcast.536), channel_id=1, replica_groups=mesh['rows'=16,'cols'=2] {'cols'}, use_global_device_ids=true, to_apply=%region_27.0 | all-reduce | flops 8192 | bytes 65536 | tf_op jit(solution)/shard_map/psum | solution.py:42
  641.2 57.6 %all-reduce.1 = (f32[16,16]{0,1:T(8,128)S(1)}, f32[16,16]{0,1:T(8,128)S(1)}) all-reduce(f32[16,16]{0,1:T(8,128)S(1)} %convolution_bitcast_fusion.10, f32[16,16]{0,1:T(8,128)S(1)} %convolution_bitcast_fusion.9), channel_id=1, replica_groups=mesh['rows'=16,'cols'=2] {'rows'}, use_global_device_ids=true, to_apply=%region_28.0 | all-reduce | flops 512 | bytes 4096 | tf_op jit(solution)/shard_map/psum | solution.py:59
  725.1 17.8 %all_gather.39 = f32[4096,16]{0,1:T(8,128)S(1)} all-gather(f32[256,16]{0,1:T(8,128)S(1)} %constant_dynamic-slice_fusion), channel_id=1, replica_groups=mesh['rows'=16,'cols'=2] {'rows'}, dimensions={0}, use_global_device_ids=true | all-gather | bytes 278528 | tf_op jit(solution)/shard_map/all_gather | solution.py:40
  744.1 7.4 psum.213
  752.1 30.1 %all-reduce = (f32[]{:T(128)}, f32[]{:T(128)}) all-reduce(f32[]{:T(128)} %get-tuple-element.1350, f32[]{:T(128)} %get-tuple-element.1349), channel_id=1, replica_groups=mesh['rows'=16,'cols'=2] {'rows'}, use_global_device_ids=true, to_apply=%region_32.0 | all-reduce | flops 2 | bytes 16 | tf_op jit(solution)/shard_map/psum | solution.py:63
  (647 shorter events, 197.6 us)
Async XLA Ops:
  0.0 35.4 %copy-start = (f32[4,2,128,128]{3,2,1,0:T(8,128)S(1)}, f32[4,2,128,128]{3,2,1,0:T(8,128)}, u32[]{:S(2)}) copy-start(f32[4,2,128,128]{3,2,1,0:T(8,128)} %param.231) | copy-start | bytes 1572868
  0.0 0.7 copy-start.3
  0.0 7.4 copy-start.1
  0.8 0.7 copy-start.4
  1.5 0.7 copy-start.2
where the time goes:
time: 786 us; the launch traced here: 784 us
  blocking collectives  575 us (73%)
  other arithmetic  106 us (13%)
  local copies, waits for them, and re-layouts  89.3 us (11%)
    psum x4, blocking collectives, per_device(): lax.psum((gram(start_rows, image), gram(start_rows, residual)), 'rows')  231 us
    all_gather x8, blocking collectives, product_of(): gathered = lax.all_gather(piece, 'rows', axis=0, tiled=True)  148 us
    psum x4, blocking collectives, per_device(): lax.psum((jnp.sum(second * middle), jnp.sum(second * second), gram(start_...  123 us
    div x112, other arithmetic, solve_block(): pivot_row = joined[index] / joined[index, index]  93.7 us
    slice x109, local copies, waits for them, and re-layouts, solve_block(): pivot_row = joined[index] / joined[index, index]  66.7 us
    psum x8, blocking collectives, product_of(): return lax.psum(total, 'cols')  62.9 us

commit v1 on v0

v1 whole, which is shorter than its diff:
```python
import functools

import jax
import jax.numpy as jnp
from jax import lax
from jax.experimental import pallas as pl
from jax.experimental.pallas import tpu as pltpu
from jax.sharding import PartitionSpec as P

ITERS = 4
MESH = pl.DeviceIdType.MESH
HIGHEST = lax.Precision.HIGHEST
NT = (((1,), (1,)), ((), ()))
NN = (((1,), (0,)), ((), ()))


def dot(left, right, dims=NN):
    return lax.dot_general(left, right, dims, precision=HIGHEST, preferred_element_type=jnp.float32)


def split(x):
    high = x.astype(jnp.bfloat16)
    rest = x - high.astype(jnp.float32)
    mid = rest.astype(jnp.bfloat16)
    low = (rest - mid.astype(jnp.float32)).astype(jnp.bfloat16)
    return high, mid, low


def right_solve(matrix, right):
    size = matrix.shape[0]
    joined = jnp.concatenate([matrix, right], axis=0)
    lane = lax.broadcasted_iota(jnp.int32, joined.shape, 1)
    for index in range(size):
        scaled = joined[:, index : index + 1] / joined[index : index + 1, index : index + 1]
        joined = jnp.where(lane == index, scaled, joined - scaled * joined[index : index + 1, :])
    return joined[size:]


def kernel(
    R, C, cols_ref, counts_ref, rhs_ref, diag_ref, blocks_ref, out_ref,
    gat0, gat1, small, part, outgoing, smallout, weights, resid, direc, image, aresid, prod, seco,
    gsend, grecv, ssend, srecv, psend, precv,
):
    PB, S, width = rhs_ref.shape
    BR, KC = blocks_ref.shape[0], blocks_ref.shape[1]
    r = lax.axis_index("rows")
    c = lax.axis_index("cols")

    gat = (gat0, gat1)

    barrier = pltpu.get_barrier_semaphore()

    def greet_row(d, carry):
        pl.semaphore_signal(barrier, inc=1, device_id=(lax.rem(r + d, R), c), device_id_type=MESH)
        return carry

    lax.fori_loop(1, R, greet_row, 0)
    for d in range(1, C):
        pl.semaphore_signal(barrier, inc=1, device_id=(r, lax.rem(c + d, C)), device_id_type=MESH)

    for b in range(BR):
        for k in range(KC):
            used = k < counts_ref[b, 0]
            block = jnp.where(used, blocks_ref[b, k], 0.0).T
            for s, piece in enumerate(split(block)):
                weights[b, s, k * width : (k + 1) * width, :] = piece

    for j in range(PB):
        gat[0][r, j] = rhs_ref[j]
        resid[j] = rhs_ref[j]
        direc[j] = rhs_ref[j]
        out_ref[j] = jnp.zeros((S, width), jnp.float32)
    gat[0][r, PB] = jnp.zeros((S, width), jnp.float32)

    pl.semaphore_wait(barrier, R - 1 + C - 1)

    def row_copy(p, dst, first, count):
        ref = gat[p].at[r, pl.ds(first, count)]
        return pltpu.make_async_remote_copy(
            src_ref=ref, dst_ref=ref, send_sem=gsend.at[dst], recv_sem=grecv.at[p, r],
            device_id=(dst, c), device_id_type=MESH,
        )

    def send_rows(p, first, count):
        def body(d, carry):
            row_copy(p, lax.rem(r + d, R), first, count).start()
            return carry
        lax.fori_loop(1, R, body, 0)

    def wait_rows(p, first, count):
        def body(d, carry):
            src = lax.rem(r + d, R)
            ref = gat[p].at[src, pl.ds(first, count)]
            pltpu.make_async_remote_copy(
                src_ref=ref, dst_ref=ref, send_sem=gsend.at[src], recv_sem=grecv.at[p, src],
                device_id=(src, c), device_id_type=MESH,
            ).wait_recv()
            return carry
        lax.fori_loop(1, R, body, 0)

    def wait_sent(p, first, count):
        def body(d, carry):
            row_copy(p, lax.rem(r + d, R), first, count).wait_send()
            return carry
        lax.fori_loop(1, R, body, 0)

    def small_copy(p, d):
        dst = lax.rem(c + d, C)
        return pltpu.make_async_remote_copy(
            src_ref=smallout.at[p], dst_ref=small.at[p, d], send_sem=ssend.at[d],
            recv_sem=srecv.at[p, d], device_id=(r, dst), device_id_type=MESH,
        )

    def part_copy(p, d):
        dst = lax.rem(c + d, C)
        return pltpu.make_async_remote_copy(
            src_ref=outgoing.at[p, d], dst_ref=part.at[p, d], send_sem=psend.at[d],
            recv_sem=precv.at[p, d], device_id=(r, dst), device_id_type=MESH,
        )

    def begin_small(p):
        total = gat[p][0, PB]
        for i in range(1, R):
            total = total + gat[p][i, PB]
        smallout[p] = total
        for d in range(1, C):
            small_copy(p, d).start()

    def end_small(p):
        total = smallout[p]
        for d in range(1, C):
            small_copy(p, d).wait()
            total = total + small[p, d]
        return total

    def block_row(p, b):
        picked = []
        for k in range(KC):
            column = cols_ref[b, k]
            picked.append(gat[p][lax.div(column, PB), lax.rem(column, PB)])
        high, mid, low = split(jnp.concatenate(picked, axis=1))
        first = jnp.concatenate([high, mid, low], axis=0)
        a = lax.dot_general(first, weights[b, 0], NN, preferred_element_type=jnp.float32)
        m = lax.dot_general(first[: 2 * S], weights[b, 1], NN, preferred_element_type=jnp.float32)
        z = lax.dot_general(first[:S], weights[b, 2], NN, preferred_element_type=jnp.float32)
        return a[:S] + ((a[S : 2 * S] + m[:S]) + ((a[2 * S :] + m[S:]) + z))

    def begin_parts(p):
        for b in range(BR):
            prod[b] = block_row(p, b)
        for d in range(1, C):
            dst = lax.rem(c + d, C)
            for j in range(PB):
                outgoing[p, d, j] = prod[dst * PB + j]
            part_copy(p, d).start()

    def end_parts(p, j):
        total = diag_ref[j] * gat[p][r, j] + prod[c * PB + j]
        for d in range(1, C):
            total = total + part[p, d, j]
        return total

    def wait_parts(p):
        for d in range(1, C):
            part_copy(p, d).wait()

    blank = jnp.zeros((S, width - 2 * S), jnp.float32)
    eye = (
        lax.broadcasted_iota(jnp.int32, (S, S), 0) == lax.broadcasted_iota(jnp.int32, (S, S), 1)
    ).astype(jnp.float32)

    send_rows(0, 0, PB + 1)
    wait_rows(0, 0, PB + 1)
    begin_parts(0)
    wait_parts(0)
    for j in range(PB):
        value = end_parts(0, j)
        image[j] = value
        aresid[j] = value
    wait_sent(0, 0, PB + 1)

    def first_half(iteration):
        mt = jnp.zeros((S, S), jnp.float32)
        gt = jnp.zeros((S, S), jnp.float32)
        for j in range(PB):
            gat[1][r, j] = image[j]
            mt = mt + dot(image[j], rhs_ref[j], NT)
            gt = gt + dot(resid[j], rhs_ref[j], NT)
        gat[1][r, PB] = jnp.concatenate([mt, gt, blank], axis=1)
        send_rows(1, 0, PB + 1)
        wait_rows(1, 0, PB + 1)
        begin_small(1)
        begin_parts(1)
        total = end_small(1)
        solved = right_solve(total[:, :S], jnp.concatenate([total[:, S : 2 * S], eye], axis=0))
        alpha, inverse = solved[:S], solved[S:]
        wait_parts(1)
        crossing = jnp.zeros((S, S), jnp.float32)
        along = jnp.zeros((S, 1), jnp.float32)
        square = jnp.zeros((S, 1), jnp.float32)
        for j in range(PB):
            moved = end_parts(1, j)
            middle = resid[j] - dot(alpha, image[j])
            second = aresid[j] - dot(alpha, moved)
            out_ref[j] = out_ref[j] + dot(alpha, direc[j])
            resid[j] = middle
            aresid[j] = moved
            seco[j] = second
            crossing = crossing + dot(second, rhs_ref[j], NT)
            along = along + jnp.sum(second * middle, axis=1, keepdims=True)
            square = square + jnp.sum(second * second, axis=1, keepdims=True)
        wait_sent(1, 0, PB + 1)
        for j in range(PB):
            gat[0][r, j] = seco[j]
        wide = (S, S)
        gat[0][r, PB] = jnp.concatenate(
            [crossing, jnp.broadcast_to(along, wide), jnp.broadcast_to(square, wide),
             jnp.zeros((S, width - 3 * S), jnp.float32)], axis=1,
        )
        return inverse

    def omega_of(total):
        sums = jnp.sum(total, axis=0, keepdims=True)
        return sums[:, S : S + 1] / sums[:, 2 * S : 2 * S + 1]

    def iterate(iteration, carry):
        inverse = first_half(iteration)
        send_rows(0, 0, PB + 1)
        wait_rows(0, 0, PB + 1)
        begin_small(0)
        begin_parts(0)
        total = end_small(0)
        omega = omega_of(total)
        beta = -dot(total[:, :S], inverse)
        for j in range(PB):
            middle = resid[j]
            out_ref[j] = out_ref[j] + omega * middle
            residual = middle - omega * seco[j]
            direc[j] = residual + dot(beta, direc[j] - omega * image[j])
            resid[j] = residual
            prod_part = image[j] - omega * aresid[j]
            image[j] = dot(beta, prod_part)
        wait_parts(0)
        for j in range(PB):
            value = seco[j] - omega * end_parts(0, j)
            aresid[j] = value
            image[j] = value + image[j]
        wait_sent(0, 0, PB + 1)
        return carry

    lax.fori_loop(0, ITERS - 1, iterate, 0)
    first_half(ITERS - 1)
    send_rows(0, PB, 1)
    wait_rows(0, PB, 1)
    begin_small(0)
    omega = omega_of(end_small(0))
    for j in range(PB):
        out_ref[j] = out_ref[j] + omega * resid[j]
    wait_sent(0, PB, 1)


def solution(mesh):
    R, C = mesh.shape["rows"], mesh.shape["cols"]

    def per_device(rhs, diagonal, blocks, block_cols, counts):
        width = blocks.shape[2]
        S = rhs.shape[1]
        PB = rhs.shape[0] // width
        BR, KC = blocks.shape[0], blocks.shape[1]
        vector = pltpu.VMEM((PB, S, width), jnp.float32)
        vmem = pl.BlockSpec(memory_space=pltpu.VMEM)
        smem = pl.BlockSpec(memory_space=pltpu.SMEM)
        out = pl.pallas_call(
            functools.partial(kernel, R, C),
            out_shape=jax.ShapeDtypeStruct((PB, S, width), jnp.float32),
            in_specs=[smem, smem, vmem, vmem, vmem],
            out_specs=vmem,
            scratch_shapes=[
                pltpu.VMEM((R, PB + 1, S, width), jnp.float32),
                pltpu.VMEM((R, PB + 1, S, width), jnp.float32),
                pltpu.VMEM((2, C, S, width), jnp.float32),
                pltpu.VMEM((2, C, PB, S, width), jnp.float32),
                pltpu.VMEM((2, C, PB, S, width), jnp.float32),
                pltpu.VMEM((2, S, width), jnp.float32),
                pltpu.VMEM((BR, 3, KC * width, width), jnp.bfloat16),
                vector, vector, vector, vector,
                pltpu.VMEM((BR, S, width), jnp.float32),
                vector,
                pltpu.SemaphoreType.DMA((R,)),
                pltpu.SemaphoreType.DMA((2, R)),
                pltpu.SemaphoreType.DMA((C,)),
                pltpu.SemaphoreType.DMA((2, C)),
                pltpu.SemaphoreType.DMA((C,)),
                pltpu.SemaphoreType.DMA((2, C)),
            ],
            compiler_params=pltpu.CompilerParams(
                collective_id=0, has_side_effects=True, vmem_limit_bytes=48 * 1024 * 1024
            ),
        )(
            block_cols, counts,
            rhs.reshape(PB, width, S).transpose(0, 2, 1),
            diagonal.reshape(PB, 1, width),
            blocks,
        )
        return out.transpose(0, 2, 1).reshape(PB * width, S)

    in_specs = (
        P(("rows", "cols"), None),
        P(("rows", "cols")),
        P("rows", "cols", None, None),
        P("rows", "cols"),
        P("rows", "cols"),
    )
    return jax.shard_map(
        per_device, mesh=mesh, in_specs=in_specs, out_specs=P(("rows", "cols"), None), check_vma=False
    )
```

time: 786 us -> 124 us (0.16)
  blocking collectives: 575 us -> 0 us
  Pallas kernels: 0 us -> 120 us
  other arithmetic: 106 us -> 0 us
  local copies, waits for them, and re-layouts: 89.3 us -> 3.77 us
    psum x16 -> x0, blocking collectives: 417 us -> none  [the longest x4 231 us: per_device(): lax.psum((gram(start_rows, image), gram(start_rows, residual)), 'rows')]
    all_gather x10 -> x0, blocking collectives: 158 us -> none  [the longest x8 148 us: product_of(): gathered = lax.all_gather(piece, 'rows', axis=0, tiled=True)]
    pallas_call x0 -> x1, Pallas kernels: none -> 120 us  [per_device(): pl.pallas_call(functools.partial(kernel, R, C), out_shape=jax.ShapeDtypeS...]
    div x112 -> x0, other arithmetic: 93.7 us -> none  [solve_block(): pivot_row = joined[index] / joined[index, index]]
    slice x109 -> x0, local copies, waits for them, and re-layouts: 66.7 us -> none  [solve_block(): pivot_row = joined[index] / joined[index, index]]
    scatter x112 -> x0, local copies, waits for them, and re-layouts: 15.4 us -> none  [solve_block(): joined = joined.at[index].set(pivot_row)]
    sub x115 -> x0, other arithmetic: 8.57 us -> none  [the longest x112 8.54 us: solve_block(): joined = joined - joined[:, index:index + 1] * pivot_row[None, :]]
where the time goes in v1:
time: 124 us; the launch traced here: 123 us
  Pallas kernels  120 us (97%)
  local copies, waits for them, and re-layouts  3.77 us (3%)
    pallas_call x1, Pallas kernels, per_device(): pl.pallas_call(functools.partial(kernel, R, C), out_shape=jax.ShapeDtypeS...  120 us
    unnamed x12, local copies, waits for them, and re-layouts  3.16 us

profile of v1, /device:TPU:0, one launch (start us, length us, event | category | flops | bytes accessed | tf_op | source)
XLA Modules:
  0.0 123.4 jit_solution(11322019202361548616)
XLA Ops:
  0.0 0.0 copy-start
  0.0 0.0 copy-start.3
  0.0 0.7 copy-done.3
  0.7 0.0 copy-start.4
  0.7 0.1 copy.9.cols_ref
  0.8 0.6 copy-done.4
  1.4 0.1 copy.10.counts_ref
  1.4 0.0 copy-done
  1.4 0.0 copy-start.2
  1.5 0.7 copy-done.2
  2.1 0.0 copy-start.1
  2.1 1.0 copy-done.1
  3.2 119.7 %shard_map.55 = f32[2,16,128]{2,1,0:T(8,128)S(1)} custom-call(s32[4,2]{1,0:T(4,128)S(1)} %copy.9.cols_ref, s32[4,1]{1,0:T(4,128)S(1)} %copy.10.counts_ref, f32[2,16,128]{2,1,0:T(8,128)S(1)} %bitcast_bitcast_fusion.rhs_ref, f32[2,1,128]{2,1,0:T(1,128)S(1)} %bitcast.14, f32[4,2,128,128]{3,2,1,0:T(8,128)S(1)} %copy-done.1), custom_call_target="tpu_custom_call" | custom-call | tf_op jit(solution)/shard_map/pallas_call | solution.py:273
  122.8 0.6 copy_bitcast_fusion
  (1 shorter events, 0.0 us)
Async XLA Ops:
  0.0 1.4 %copy-start = (f32[256,16]{0,1:T(8,128)S(1)}, f32[256,16]{0,1:T(8,128)}, u32[]{:S(2)}) copy-start(f32[256,16]{0,1:T(8,128)} %param.5) | copy-start | bytes 49156
  0.0 0.7 copy-start.3
  0.7 0.7 copy-start.4
  1.4 0.7 copy-start.2
  2.1 1.0 copy-start.1

commit v2 on v1

v2 whole, which is shorter than its diff:
```python
import functools

import jax
import jax.numpy as jnp
from jax import lax
from jax.experimental import pallas as pl
from jax.experimental.pallas import tpu as pltpu
from jax.sharding import PartitionSpec as P

ITERS = 4
H = 2
TILE = 8
MESH = pl.DeviceIdType.MESH
HIGHEST = lax.Precision.HIGHEST
NT = (((1,), (1,)), ((), ()))
NN = (((1,), (0,)), ((), ()))


def dot(left, right, dims=NN):
    return lax.dot_general(left, right, dims, precision=HIGHEST, preferred_element_type=jnp.float32)


def split(x):
    high = x.astype(jnp.bfloat16)
    rest = x - high.astype(jnp.float32)
    mid = rest.astype(jnp.bfloat16)
    low = (rest - mid.astype(jnp.float32)).astype(jnp.bfloat16)
    return high, mid, low


def right_solve(matrix, right):
    size = matrix.shape[0]
    joined = jnp.concatenate([matrix, right], axis=0)
    lane = lax.broadcasted_iota(jnp.int32, joined.shape, 1)
    for index in range(size):
        scaled = joined[:, index : index + 1] / joined[index : index + 1, index : index + 1]
        joined = jnp.where(lane == index, scaled, joined - scaled * joined[index : index + 1, :])
    return joined[size:]


def kernel(
    R, C, meta_hbm, rhs_hbm, diag_hbm, blocks_hbm, out_ref,
    gat0, gat1, pay, small, part, outgoing, smallout, weights, raw, metav, metas,
    rhs_ref, diag_ref, resid, direc, image, aresid, prod, seco, sums,
    local, mine, theirs, gsend, grecv, ysend, yrecv, ssend, srecv, psend, precv,
):
    PB, S, width = rhs_ref.shape
    BR, KC = raw.shape[1], raw.shape[2]
    RG = R // H
    r = lax.axis_index("rows")
    c = lax.axis_index("cols")
    h = lax.rem(r, H)
    g = lax.div(r, H)
    gat = (gat0, gat1)
    peers = [(dh, d) for dh in range(H) for d in range(C) if (dh, d) != (0, 0)]

    def row_of(d):
        return lax.rem(g + d, RG)

    def peer(dh, d):
        return (g * H + lax.rem(h + dh, H), lax.rem(c + d, C))

    barrier = pltpu.get_barrier_semaphore()

    def greet(d, carry):
        pl.semaphore_signal(barrier, inc=1, device_id=(row_of(d) * H + h, c), device_id_type=MESH)
        return carry

    lax.fori_loop(1, RG, greet, 0)
    for dh, d in peers:
        pl.semaphore_signal(barrier, inc=1, device_id=peer(dh, d), device_id_type=MESH)

    take_rhs = pltpu.make_async_copy(rhs_hbm, rhs_ref, local.at[0])
    take_blocks = pltpu.make_async_copy(blocks_hbm, raw.at[0], local.at[1])
    take_meta = pltpu.make_async_copy(meta_hbm, metav.at[0], local.at[2])
    take_diag = pltpu.make_async_copy(diag_hbm, diag_ref, local.at[3])
    for copy in (take_rhs, take_meta, take_blocks, take_diag):
        copy.start()
    take_rhs.wait()
    for j in range(PB):
        gat0[g, j] = rhs_ref[j]
        resid[j] = rhs_ref[j]
        direc[j] = rhs_ref[j]
        out_ref[j] = jnp.zeros((S, width), jnp.float32)
    take_meta.wait()
    pltpu.make_async_copy(metav.at[0], metas.at[0], local.at[2]).start()
    take_blocks.wait()

    pl.semaphore_wait(barrier, RG - 1 + H * C - 1)

    def row_copy(p, src, dst):
        ref = gat[p].at[src]
        return pltpu.make_async_remote_copy(
            src_ref=ref, dst_ref=ref, send_sem=gsend.at[dst], recv_sem=grecv.at[p, src],
            device_id=(dst * H + h, c), device_id_type=MESH,
        )

    def pay_copy(p, src, dst):
        ref = pay.at[p, src]
        return pltpu.make_async_remote_copy(
            src_ref=ref, dst_ref=ref, send_sem=ysend.at[dst], recv_sem=yrecv.at[p, src],
            device_id=(dst * H + h, c), device_id_type=MESH,
        )

    def each(action):
        def body(d, carry):
            action(row_of(d))
            return carry
        lax.fori_loop(1, RG, body, 0)

    def send(copy, p):
        each(lambda other: copy(p, g, other).start())

    def receive(copy, p):
        each(lambda other: copy(p, other, other).wait_recv())

    def sent(copy, p):
        each(lambda other: copy(p, g, other).wait_send())

    def peer_copy(source, target, send_sem, recv_sem, dh, d):
        return pltpu.make_async_remote_copy(
            src_ref=source, dst_ref=target, send_sem=send_sem, recv_sem=recv_sem,
            device_id=peer(dh, d), device_id_type=MESH,
        )

    def small_copy(p, dh, d):
        e = dh * C + d
        return peer_copy(smallout.at[p], small.at[p, e], ssend.at[e], srecv.at[p, e], dh, d)

    def part_copy(p, dh, d):
        e = dh * C + d
        return peer_copy(outgoing.at[p, e], part.at[p, e], psend.at[e], precv.at[p, e], dh, d)

    def begin_small(p):
        total = pay[p, 0]
        for i in range(1, RG):
            total = total + pay[p, i]
        smallout[p] = total
        for dh, d in peers:
            small_copy(p, dh, d).start()

    def end_small(p):
        total = smallout[p]
        for dh, d in peers:
            small_copy(p, dh, d).wait()
            total = total + small[p, dh * C + d]
        return total

    def block_row(p, hh, b):
        picked = []
        for k in range(KC):
            column = metas[hh, 0, b * KC + k]
            owner = lax.div(lax.div(column, PB), H)
            picked.append(gat[p][owner, lax.rem(column, PB)])
        high, mid, low = split(jnp.concatenate(picked, axis=1))
        first = jnp.concatenate([high, mid, low], axis=0)
        a = lax.dot_general(first, weights[hh, b, 0], NN, preferred_element_type=jnp.float32)
        m = lax.dot_general(first[: 2 * S], weights[hh, b, 1], NN, preferred_element_type=jnp.float32)
        z = lax.dot_general(first[:S], weights[hh, b, 2], NN, preferred_element_type=jnp.float32)
        return a[:S] + ((a[S : 2 * S] + m[:S]) + ((a[2 * S :] + m[S:]) + z))

    def begin_parts(p):
        for hh in range(H):
            for b in range(BR):
                prod[hh, b] = block_row(p, hh, b)
        for dh, d in peers:
            e = dh * C + d
            for j in range(PB):
                outgoing[p, e, j] = prod[dh, lax.rem(c + d, C) * PB + j]
            part_copy(p, dh, d).start()

    def wait_parts(p):
        for dh, d in peers:
            part_copy(p, dh, d).wait()

    def end_parts(p, j):
        total = diag_ref[j] * gat[p][g, j] + prod[0, c * PB + j]
        for dh, d in peers:
            total = total + part[p, dh * C + d, j]
        return total

    def prepare(hh):
        for b in range(BR):
            for k in range(KC):
                column = metas[hh, 0, b * KC + k]
                count = metas[hh, 0, BR * KC + b]
                here = (k < count) & (lax.rem(lax.div(column, PB), H) == h)
                block = jnp.where(here, raw[hh, b, k], 0.0).T
                for s, piece in enumerate(split(block)):
                    weights[hh, b, s, k * width : (k + 1) * width, :] = piece

    send(row_copy, 0)
    swap_meta = peer_copy(metav.at[0], metav.at[1], mine.at[0], theirs.at[0], 1, 0)
    swap_blocks = peer_copy(raw.at[0], raw.at[1], mine.at[1], theirs.at[1], 1, 0)
    swap_meta.start()
    swap_blocks.start()
    pltpu.make_async_copy(metav.at[0], metas.at[0], local.at[2]).wait()
    swap_meta.wait()
    second_meta = pltpu.make_async_copy(metav.at[1], metas.at[1], local.at[2])
    second_meta.start()
    second_meta.wait()

    prepare(0)
    swap_blocks.wait()
    prepare(1)
    take_diag.wait()
    receive(row_copy, 0)
    begin_parts(0)
    wait_parts(0)
    for j in range(PB):
        value = end_parts(0, j)
        image[j] = value
        aresid[j] = value
    sent(row_copy, 0)

    eye = (
        lax.broadcasted_iota(jnp.int32, (S, S), 0) == lax.broadcasted_iota(jnp.int32, (S, S), 1)
    ).astype(jnp.float32)

    def flat(matrix):
        return [matrix[i : i + TILE] for i in range(0, S, TILE)]

    def unflat(total, first):
        count = S // TILE
        return jnp.concatenate(
            [total[:, first + i * S : first + (i + 1) * S] for i in range(count)], axis=0
        )

    def tile(parts):
        used = sum(x.shape[1] for x in parts)
        return jnp.concatenate(parts + [jnp.zeros((TILE, width - used), jnp.float32)], axis=1)

    half = S * (S // TILE)

    def first_half():
        for j in range(PB):
            gat1[g, j] = image[j]
        send(row_copy, 1)
        mt = jnp.zeros((S, S), jnp.float32)
        gt = jnp.zeros((S, S), jnp.float32)
        for j in range(PB):
            mt = mt + dot(image[j], rhs_ref[j], NT)
            gt = gt + dot(resid[j], rhs_ref[j], NT)
        pay[1, g] = tile(flat(mt) + flat(gt))
        send(pay_copy, 1)
        receive(pay_copy, 1)
        begin_small(1)
        receive(row_copy, 1)
        begin_parts(1)
        total = end_small(1)
        solved = right_solve(unflat(total, 0), jnp.concatenate([unflat(total, half), eye], axis=0))
        alpha, inverse = solved[:S], solved[S:]
        for j in range(PB):
            resid[j] = resid[j] - dot(alpha, image[j])
            out_ref[j] = out_ref[j] + dot(alpha, direc[j])
        sent(row_copy, 1)
        sent(pay_copy, 1)
        wait_parts(1)
        for j in range(PB):
            moved = end_parts(1, j)
            second = aresid[j] - dot(alpha, moved)
            aresid[j] = moved
            seco[j] = second
            gat0[g, j] = second
        return inverse

    def offer_second():
        crossing = jnp.zeros((S, S), jnp.float32)
        along = jnp.zeros((S, 1), jnp.float32)
        square = jnp.zeros((S, 1), jnp.float32)
        for j in range(PB):
            second = seco[j]
            crossing = crossing + dot(second, rhs_ref[j], NT)
            along = along + jnp.sum(second * resid[j], axis=1, keepdims=True)
            square = square + jnp.sum(second * second, axis=1, keepdims=True)
        wide = (TILE, S)
        pay[0, g] = tile(
            flat(crossing)
            + [jnp.broadcast_to(sum(flat(along)), wide), jnp.broadcast_to(sum(flat(square)), wide)]
        )
        send(pay_copy, 0)
        receive(pay_copy, 0)
        begin_small(0)

    def omega_of(total):
        line = jnp.sum(total, axis=0, keepdims=True)
        return line[:, half : half + 1] / line[:, half + S : half + S + 1]

    def iterate(iteration, carry):
        inverse = first_half()
        send(row_copy, 0)
        offer_second()
        receive(row_copy, 0)
        begin_parts(0)
        total = end_small(0)
        omega = omega_of(total)
        beta = -dot(unflat(total, 0), inverse)
        for j in range(PB):
            middle = resid[j]
            out_ref[j] = out_ref[j] + omega * middle
            residual = middle - omega * seco[j]
            direc[j] = residual + dot(beta, direc[j] - omega * image[j])
            resid[j] = residual
            sums[j] = seco[j] + dot(beta, image[j] - omega * aresid[j])
        sent(row_copy, 0)
        sent(pay_copy, 0)
        wait_parts(0)
        for j in range(PB):
            moved = omega * end_parts(0, j)
            aresid[j] = seco[j] - moved
            image[j] = sums[j] - moved
        return carry

    lax.fori_loop(0, ITERS - 1, iterate, 0)
    first_half()
    offer_second()
    omega = omega_of(end_small(0))
    for j in range(PB):
        out_ref[j] = out_ref[j] + omega * resid[j]
    sent(pay_copy, 0)


def solution(mesh):
    R, C = mesh.shape["rows"], mesh.shape["cols"]

    def per_device(rhs, diagonal, blocks, block_cols, counts):
        width = blocks.shape[2]
        S = rhs.shape[1]
        PB = rhs.shape[0] // width
        BR, KC = blocks.shape[0], blocks.shape[1]
        RG, E = R // H, H * C
        f32 = jnp.float32
        vector = pltpu.VMEM((PB, S, width), f32)
        hbm = pl.BlockSpec(memory_space=pltpu.HBM)
        vmem = pl.BlockSpec(memory_space=pltpu.VMEM)
        dma = pltpu.SemaphoreType.DMA
        numbers = jnp.concatenate([block_cols.reshape(-1), counts.reshape(-1)])
        meta = jnp.pad(numbers[None, :], ((0, TILE - 1), (0, width - numbers.shape[0])))
        out = pl.pallas_call(
            functools.partial(kernel, R, C),
            out_shape=jax.ShapeDtypeStruct((PB, S, width), f32),
            in_specs=[hbm, hbm, hbm, hbm],
            out_specs=vmem,
            scratch_shapes=[
                pltpu.VMEM((RG, PB, S, width), f32),
                pltpu.VMEM((RG, PB, S, width), f32),
                pltpu.VMEM((2, RG, TILE, width), f32),
                pltpu.VMEM((2, E, TILE, width), f32),
                pltpu.VMEM((2, E, PB, S, width), f32),
                pltpu.VMEM((2, E, PB, S, width), f32),
                pltpu.VMEM((2, TILE, width), f32),
                pltpu.VMEM((H, BR, 3, KC * width, width), jnp.bfloat16),
                pltpu.VMEM((H, BR, KC, width, width), f32),
                pltpu.VMEM((H, TILE, width), jnp.int32),
                pltpu.SMEM((H, TILE, width), jnp.int32),
                vector,
                pltpu.VMEM((PB, 1, width), f32),
                vector, vector, vector, vector,
                pltpu.VMEM((H, BR, S, width), f32),
                vector, vector,
                dma((4,)), dma((2,)), dma((2,)),
                dma((RG,)), dma((2, RG)),
                dma((RG,)), dma((2, RG)),
                dma((E,)), dma((2, E)),
                dma((E,)), dma((2, E)),
            ],
            compiler_params=pltpu.CompilerParams(
                collective_id=0, has_side_effects=True, vmem_limit_bytes=48 * 1024 * 1024
            ),
        )(
            meta,
            rhs.reshape(PB, width, S).transpose(0, 2, 1),
            diagonal.reshape(PB, 1, width),
            blocks,
        )
        return out.transpose(0, 2, 1).reshape(PB * width, S)

    in_specs = (
        P(("rows", "cols"), None),
        P(("rows", "cols")),
        P("rows", "cols", None, None),
        P("rows", "cols"),
        P("rows", "cols"),
    )
    return jax.shard_map(
        per_device, mesh=mesh, in_specs=in_specs, out_specs=P(("rows", "cols"), None), check_vma=False
    )
```

time: 124 us -> 94.4 us (0.76)
  Pallas kernels: 120 us -> 90.3 us
    pallas_call x1, Pallas kernels: 120 us -> 90.3 us  [per_device(): pl.pallas_call(functools.partial(kernel, R, C), out_shape=jax.ShapeDtypeS...]
    unnamed x12 -> x11, local copies, waits for them, and re-layouts: 3.16 us -> 3.07 us
where the time goes in v2:
time: 94.4 us; the launch traced here: 94.1 us
  Pallas kernels  90.3 us (96%)
  local copies, waits for them, and re-layouts  3.77 us (4%)
    pallas_call x1, Pallas kernels, per_device(): pl.pallas_call(functools.partial(kernel, R, C), out_shape=jax.ShapeDtypeS...  90.3 us
    unnamed x11, local copies, waits for them, and re-layouts  3.07 us

profile of v2, /device:TPU:0, one launch (start us, length us, event | category | flops | bytes accessed | tf_op | source)
XLA Modules:
  0.0 94.1 jit_solution(9839872322627356465)
XLA Ops:
  0.0 0.0 copy-start
  0.0 0.0 copy-start.3
  0.0 0.7 copy-done.3
  0.7 0.1 copy.7
  0.8 0.0 copy-start.4
  0.8 0.1 reshape.15
  0.9 0.6 copy-done.4
  1.4 0.1 add_bitcast_fusion
  1.5 0.0 copy-done
  1.5 0.0 copy-start.2
  1.5 0.7 copy-done.2
  2.2 0.0 copy-start.1
  2.2 1.0 %copy-done.1 = f32[4,2,128,128]{3,2,1,0:T(8,128)S(1)} copy-done((f32[4,2,128,128]{3,2,1,0:T(8,128)S(1)}, f32[4,2,128,128]{3,2,1,0:T(8,128)}, u32[]{:S(2)}) %copy-start.1) | copy-done | bytes 524312
  3.3 90.3 %shard_map.55 = f32[2,16,128]{2,1,0:T(8,128)S(1)} custom-call(s32[8,128]{1,0:T(8,128)S(1)} %pad.4.meta_hbm, f32[2,16,128]{2,1,0:T(8,128)S(1)} %bitcast_bitcast_fusion.rhs_hbm, f32[2,1,128]{2,1,0:T(1,128)S(1)} %bitcast.17, f32[4,2,128,128]{3,2,1,0:T(8,128)S(1)} %copy-done.1), custom_call_target="tpu_custom_call" | custom-call | tf_op jit(solution)/shard_map/pallas_call | solution.py:339
  93.5 0.6 copy_bitcast_fusion
  (2 shorter events, 0.0 us)
Async XLA Ops:
  0.0 1.5 %copy-start = (f32[256,16]{0,1:T(8,128)S(1)}, f32[256,16]{0,1:T(8,128)}, u32[]{:S(2)}) copy-start(f32[256,16]{0,1:T(8,128)} %param.5) | copy-start | bytes 49156
  0.0 0.7 copy-start.3
  0.8 0.7 copy-start.4
  1.5 0.7 copy-start.2
  2.2 1.0 %copy-start.1 = (f32[4,2,128,128]{3,2,1,0:T(8,128)S(1)}, f32[4,2,128,128]{3,2,1,0:T(8,128)}, u32[]{:S(2)}) copy-start(f32[4,2,128,128]{3,2,1,0:T(8,128)} %blocks_hbm.1) | copy-start | bytes 1572868

commit v3 on v2

v3 whole, which is shorter than its diff:
```python
import functools

import jax
import jax.numpy as jnp
from jax import lax
from jax.experimental import pallas as pl
from jax.experimental.pallas import tpu as pltpu
from jax.sharding import PartitionSpec as P

ITERS = 4
H = 2
TILE = 8
MESH = pl.DeviceIdType.MESH
HIGHEST = lax.Precision.HIGHEST
NT = (((1,), (1,)), ((), ()))
NN = (((1,), (0,)), ((), ()))


def dot(left, right, dims=NN):
    return lax.dot_general(left, right, dims, precision=HIGHEST, preferred_element_type=jnp.float32)


def split(x):
    high = x.astype(jnp.bfloat16)
    rest = x - high.astype(jnp.float32)
    mid = rest.astype(jnp.bfloat16)
    low = (rest - mid.astype(jnp.float32)).astype(jnp.bfloat16)
    return high, mid, low


def right_solve(matrix, right):
    size = matrix.shape[0]
    joined = jnp.concatenate([matrix, right], axis=0)
    lane = lax.broadcasted_iota(jnp.int32, joined.shape, 1)
    for index in range(size):
        scaled = joined[:, index : index + 1] / joined[index : index + 1, index : index + 1]
        joined = jnp.where(lane == index, scaled, joined - scaled * joined[index : index + 1, :])
    return joined[size:]


def kernel(
    R, C, cols_hbm, counts_hbm, rhs_hbm, diag_hbm, blocks_hbm, out_ref,
    gat0, gat1, pay, small, smallout, part, outgoing, weights, raw, colsv, countsv, colss, countss,
    rhs_raw, rhs_ref, diag_ref, resid, direc, image, aresid, prod, seco, sums, xs, gram,
    local, mine, theirs, gsend, grecv, ysend, yrecv, ssend, srecv, psend, precv,
):
    PB, S, width = rhs_ref.shape
    BR, KC = raw.shape[1], raw.shape[2]
    RG = R // H
    N = R * C
    r = lax.axis_index("rows")
    c = lax.axis_index("cols")
    h = lax.rem(r, H)
    g = lax.div(r, H)
    gat = (gat0, gat1)
    me = r * C + c
    peers = [(dh, d) for dh in range(H) for d in range(C) if (dh, d) != (0, 0)]

    def wrap(value, count):
        return jnp.where(value >= count, value - count, value)

    groups = [wrap(g + d, RG) for d in range(RG)]
    halves = [wrap(h + d, H) for d in range(H)]
    columns = [wrap(c + d, C) for d in range(C)]
    row_devices = [(groups[d] * H + h, c) for d in range(1, RG)]
    devices = [
        (groups[i] * H + halves[j], columns[k])
        for i in range(RG) for j in range(H) for k in range(C) if (i, j, k) != (0, 0, 0)
    ]

    near = row_devices
    rest = peers
    NP, mine_slot = RG, g

    def peer(dh, d):
        return (g * H + halves[dh], columns[d])

    barrier = pltpu.get_barrier_semaphore()

    for device in devices:
        pl.semaphore_signal(barrier, inc=1, device_id=device, device_id_type=MESH)

    take_rhs = pltpu.make_async_copy(rhs_hbm, rhs_raw, local.at[0])
    take_blocks = pltpu.make_async_copy(blocks_hbm, raw.at[0], local.at[1])
    take_cols = pltpu.make_async_copy(cols_hbm, colsv.at[0], local.at[2])
    take_counts = pltpu.make_async_copy(counts_hbm, countsv.at[0], local.at[4])
    take_diag = pltpu.make_async_copy(diag_hbm, diag_ref, local.at[3])
    for copy in (take_rhs, take_cols, take_counts, take_blocks, take_diag):
        copy.start()
    take_rhs.wait()
    for j in range(PB):
        own = rhs_raw[:, j * width : (j + 1) * width]
        rhs_ref[j] = own
        gat0[g, j] = own
        resid[j] = own
        direc[j] = own
        xs[j] = jnp.zeros((S, width), jnp.float32)

    def to_scalars(i):
        first = pltpu.make_async_copy(colsv.at[i], colss.at[i], local.at[2])
        other = pltpu.make_async_copy(countsv.at[i], countss.at[i], local.at[4])
        first.start()
        other.start()
        first.wait()
        other.wait()

    take_cols.wait()
    take_counts.wait()
    to_scalars(0)
    take_blocks.wait()

    pl.semaphore_wait(barrier, N - 1)

    def broadcast(ref, send_sem, recv_sem, targets):
        for device in targets:
            pltpu.make_async_remote_copy(
                src_ref=ref, dst_ref=ref, send_sem=send_sem, recv_sem=recv_sem,
                device_id=device, device_id_type=MESH,
            ).start()

    def all_of(ref, send_sem, recv_sem):
        return pltpu.make_async_remote_copy(
            src_ref=ref, dst_ref=ref, send_sem=send_sem, recv_sem=recv_sem,
            device_id=row_devices[0], device_id_type=MESH,
        )

    def send(p):
        broadcast(gat[p].at[g], gsend.at[p], grecv.at[p], row_devices)

    def rows_copied(p):
        return all_of(gat[p].at[pl.ds(0, RG - 1)], gsend.at[p], grecv.at[p])

    def receive(p):
        rows_copied(p).wait_recv()

    def sent(p):
        rows_copied(p).wait_send()

    def pay_send(p):
        broadcast(pay.at[p, mine_slot], ysend.at[p], yrecv.at[p], near)

    def pay_copied(p):
        return all_of(pay.at[p, pl.ds(0, NP - 1)], ysend.at[p], yrecv.at[p])

    def pay_sent(p):
        pay_copied(p).wait_send()

    def peer_copy(source, target, send_sem, recv_sem, dh, d):
        return pltpu.make_async_remote_copy(
            src_ref=source, dst_ref=target, send_sem=send_sem, recv_sem=recv_sem,
            device_id=peer(dh, d), device_id_type=MESH,
        )

    def small_copy(p, dh, d):
        e = dh * C + d
        return peer_copy(smallout.at[p], small.at[p, e], ssend.at[e], srecv.at[p, e], dh, d)

    def pay_half(p):
        pay_copied(p).wait_recv()
        values = [pay[p, i] for i in range(NP)]
        while len(values) > 1:
            values = [sum(values[i : i + 2]) for i in range(0, len(values), 2)]
        smallout[p] = values[0]
        for dh, d in rest:
            small_copy(p, dh, d).start()

    def pay_total(p):
        total = smallout[p]
        for dh, d in rest:
            small_copy(p, dh, d).wait()
            total = total + small[p, dh * C + d]
        return total

    def part_copy(p, dh, d):
        e = dh * C + d
        return peer_copy(outgoing.at[p, e], part.at[p, e], psend.at[e], precv.at[p, e], dh, d)

    def block_row(p, hh, b):
        picked = []
        for k in range(KC):
            column = colss[hh, b, k]
            owner = lax.div(lax.div(column, PB), H)
            picked.append(gat[p][owner, lax.rem(column, PB)])
        high, mid, low = split(jnp.concatenate(picked, axis=1))
        first = jnp.concatenate([high, mid, low], axis=0)
        a = lax.dot_general(first, weights[hh, b, 0], NN, preferred_element_type=jnp.float32)
        m = lax.dot_general(first[: 2 * S], weights[hh, b, 1], NN, preferred_element_type=jnp.float32)
        z = lax.dot_general(first[:S], weights[hh, b, 2], NN, preferred_element_type=jnp.float32)
        return a[:S] + ((a[S : 2 * S] + m[:S]) + ((a[2 * S :] + m[S:]) + z))

    def begin_parts(p):
        for dh, d in sorted(peers, key=lambda at: at[1] == 0):
            e = dh * C + d
            for j in range(PB):
                outgoing[p, e, j] = block_row(p, dh, columns[d] * PB + j)
            part_copy(p, dh, d).start()
        for j in range(PB):
            prod[j] = block_row(p, 0, c * PB + j)

    def wait_parts(p):
        for dh, d in peers:
            part_copy(p, dh, d).wait()

    def end_parts(p, j):
        total = diag_ref[j] * gat[p][g, j] + prod[j]
        for dh, d in peers:
            total = total + part[p, dh * C + d, j]
        return total

    def prepare(hh):
        for b in range(BR):
            for k in range(KC):
                column = colss[hh, b, k]
                count = countss[hh, b, 0]
                here = (k < count) & (lax.rem(lax.div(column, PB), H) == h)
                block = jnp.where(here, raw[hh, b, k], 0.0).T
                for s, piece in enumerate(split(block)):
                    weights[hh, b, s, k * width : (k + 1) * width, :] = piece

    send(0)
    swaps = [
        peer_copy(ref.at[0], ref.at[1], mine.at[i], theirs.at[i], 1, 0)
        for i, ref in enumerate((colsv, countsv, raw))
    ]
    for swap in swaps:
        swap.start()
    gram[...] = dot(rhs_raw[...], rhs_raw[...], NT)
    prepare(0)
    for swap in swaps:
        swap.wait()
    to_scalars(1)
    prepare(1)
    take_diag.wait()
    receive(0)
    begin_parts(0)
    wait_parts(0)
    for j in range(PB):
        value = end_parts(0, j)
        image[j] = value
        aresid[j] = value
    sent(0)

    eye = (
        lax.broadcasted_iota(jnp.int32, (S, S), 0) == lax.broadcasted_iota(jnp.int32, (S, S), 1)
    ).astype(jnp.float32)

    def flat(matrix):
        return [matrix[i : i + TILE] for i in range(0, S, TILE)]

    def unflat(total, first):
        count = S // TILE
        return jnp.concatenate(
            [total[:, first + i * S : first + (i + 1) * S] for i in range(count)], axis=0
        )

    def tile(parts):
        used = sum(x.shape[1] for x in parts)
        return jnp.concatenate(parts + [jnp.zeros((TILE, width - used), jnp.float32)], axis=1)

    half = S * (S // TILE)

    def first_half():
        held = [image[j] for j in range(PB)]
        for j in range(PB):
            gat1[g, j] = held[j]
        mt = dot(jnp.concatenate(held, axis=1), rhs_raw[...], NT)
        pay[1, mine_slot] = tile(flat(mt) + flat(gram[...]))
        pay_send(1)
        send(1)
        pay_half(1)
        receive(1)
        begin_parts(1)
        total = pay_total(1)
        solved = right_solve(unflat(total, 0), jnp.concatenate([unflat(total, half), eye], axis=0))
        alpha, inverse = solved[:S], solved[S:]
        for j in range(PB):
            resid[j] = resid[j] - dot(alpha, image[j])
            xs[j] = xs[j] + dot(alpha, direc[j])
        sent(1)
        pay_sent(1)
        wait_parts(1)
        for j in range(PB):
            moved = end_parts(1, j)
            second = aresid[j] - dot(alpha, moved)
            aresid[j] = moved
            seco[j] = second
            gat0[g, j] = second
        return inverse

    def offer_second():
        along = jnp.zeros((S, 1), jnp.float32)
        square = jnp.zeros((S, 1), jnp.float32)
        held = [seco[j] for j in range(PB)]
        crossing = dot(jnp.concatenate(held, axis=1), rhs_raw[...], NT)
        for j in range(PB):
            along = along + jnp.sum(held[j] * resid[j], axis=1, keepdims=True)
            square = square + jnp.sum(held[j] * held[j], axis=1, keepdims=True)
        wide = (TILE, S)
        pay[0, mine_slot] = tile(
            flat(crossing)
            + [jnp.broadcast_to(sum(flat(along)), wide), jnp.broadcast_to(sum(flat(square)), wide)]
        )
        pay_send(0)

    def omega_of(total):
        line = jnp.sum(total, axis=0, keepdims=True)
        return line[:, half : half + 1] / line[:, half + S : half + S + 1]

    def iterate(iteration, carry):
        inverse = first_half()
        offer_second()
        send(0)
        pay_half(0)
        receive(0)
        begin_parts(0)
        total = pay_total(0)
        omega = omega_of(total)
        beta = -dot(unflat(total, 0), inverse)
        for j in range(PB):
            middle = resid[j]
            xs[j] = xs[j] + omega * middle
            residual = middle - omega * seco[j]
            direc[j] = residual + dot(beta, direc[j] - omega * image[j])
            resid[j] = residual
            sums[j] = seco[j] + dot(beta, image[j] - omega * aresid[j])
        gram[...] = dot(jnp.concatenate([resid[j] for j in range(PB)], axis=1), rhs_raw[...], NT)
        sent(0)
        pay_sent(0)
        wait_parts(0)
        for j in range(PB):
            moved = omega * end_parts(0, j)
            aresid[j] = seco[j] - moved
            image[j] = sums[j] - moved
        return carry

    lax.fori_loop(0, ITERS - 1, iterate, 0)
    first_half()
    offer_second()
    pay_half(0)
    omega = omega_of(pay_total(0))
    for j in range(PB):
        out_ref[:, j * width : (j + 1) * width] = xs[j] + omega * resid[j]
    pay_sent(0)


def solution(mesh):
    R, C = mesh.shape["rows"], mesh.shape["cols"]

    def per_device(rhs, diagonal, blocks, block_cols, counts):
        width = blocks.shape[2]
        S = rhs.shape[1]
        PB = rhs.shape[0] // width
        BR, KC = blocks.shape[0], blocks.shape[1]
        RG, E, N = R // H, H * C, R * C
        f32 = jnp.float32
        vector = pltpu.VMEM((PB, S, width), f32)
        hbm = pl.BlockSpec(memory_space=pltpu.HBM)
        vmem = pl.BlockSpec(memory_space=pltpu.VMEM)
        dma = pltpu.SemaphoreType.DMA
        out = pl.pallas_call(
            functools.partial(kernel, R, C),
            out_shape=jax.ShapeDtypeStruct((S, PB * width), f32),
            in_specs=[hbm] * 5,
            out_specs=vmem,
            scratch_shapes=[
                pltpu.VMEM((RG, PB, S, width), f32),
                pltpu.VMEM((RG, PB, S, width), f32),
                pltpu.VMEM((2, RG, TILE, width), f32),
                pltpu.VMEM((2, E, TILE, width), f32),
                pltpu.VMEM((2, TILE, width), f32),
                pltpu.VMEM((2, E, PB, S, width), f32),
                pltpu.VMEM((2, E, PB, S, width), f32),
                pltpu.VMEM((H, BR, 3, KC * width, width), jnp.bfloat16),
                pltpu.VMEM((H, BR, KC, width, width), f32),
                pltpu.VMEM((H, BR, KC), jnp.int32),
                pltpu.VMEM((H, BR, 1), jnp.int32),
                pltpu.SMEM((H, BR, KC), jnp.int32),
                pltpu.SMEM((H, BR, 1), jnp.int32),
                pltpu.VMEM((S, PB * width), f32),
                vector,
                pltpu.VMEM((PB, 1, width), f32),
                vector, vector, vector, vector,
                vector, vector, vector, vector,
                pltpu.VMEM((S, S), f32),
                dma((5,)), dma((3,)), dma((3,)),
                dma((2,)), dma((2,)),
                dma((2,)), dma((2,)),
                dma((E,)), dma((2, E)),
                dma((E,)), dma((2, E)),
            ],
            compiler_params=pltpu.CompilerParams(
                collective_id=0, has_side_effects=True, vmem_limit_bytes=48 * 1024 * 1024
            ),
        )(
            block_cols, counts, rhs.T,
            diagonal.reshape(PB, 1, width),
            blocks,
        )
        return out.T

    in_specs = (
        P(("rows", "cols"), None),
        P(("rows", "cols")),
        P("rows", "cols", None, None),
        P("rows", "cols"),
        P("rows", "cols"),
    )
    return jax.shard_map(
        per_device, mesh=mesh, in_specs=in_specs, out_specs=P(("rows", "cols"), None), check_vma=False
    )
```

time: 94.4 us -> 89.3 us (0.946)
  Pallas kernels: 90.3 us -> 84.6 us
    pallas_call x1, Pallas kernels: 90.3 us -> 84.6 us  [per_device(): pl.pallas_call(functools.partial(kernel, R, C), out_shape=jax.ShapeDtypeS...]
    unnamed x11 -> x13, local copies, waits for them, and re-layouts: 3.07 us -> 4.38 us
where the time goes in v3:
time: 89.3 us; the launch traced here: 89 us
  Pallas kernels  84.6 us (95%)
  local copies, waits for them, and re-layouts  4.38 us (5%)
    pallas_call x1, Pallas kernels, per_device(): pl.pallas_call(functools.partial(kernel, R, C), out_shape=jax.ShapeDtypeS...  84.6 us
    unnamed x13, local copies, waits for them, and re-layouts  4.38 us

profile of v3, /device:TPU:0, one launch (start us, length us, event | category | flops | bytes accessed | tf_op | source)
XLA Modules:
  0.0 89.0 jit_solution(8009405866896983598)
XLA Ops:
  0.0 0.0 copy-start.3
  0.0 0.7 copy-done.3
  0.7 0.0 copy-start.4
  0.7 0.1 copy.6.cols_hbm
  0.8 0.6 copy-done.4
  1.3 0.0 copy-start.2
  1.3 0.1 copy.7.counts_hbm
  1.4 0.6 copy-done.2
  2.0 0.0 copy-start
  2.0 1.0 %copy-done = f32[4,2,128,128]{3,2,1,0:T(8,128)S(1)} copy-done((f32[4,2,128,128]{3,2,1,0:T(8,128)S(1)}, f32[4,2,128,128]{3,2,1,0:T(8,128)}, u32[]{:S(2)}) %copy-start) | copy-done | bytes 524312
  3.1 0.0 copy-start.1
  3.1 0.7 copy-done.1
  3.8 84.6 %shard_map.55 = f32[16,256]{1,0:T(8,128)S(1)} custom-call(s32[4,2]{1,0:T(4,128)S(1)} %copy.6.cols_hbm, s32[4,1]{1,0:T(4,128)S(1)} %copy.7.counts_hbm, f32[16,256]{1,0:T(8,128)S(1)} %bitcast.4, f32[2,1,128]{2,1,0:T(1,128)S(1)} %bitcast.5, f32[4,2,128,128]{3,2,1,0:T(8,128)S(1)} %copy-done), custom_call_target="tpu_custom_call" | custom-call | tf_op jit(solution)/shard_map/pallas_call | solution.py:360
  88.4 0.6 copy.9
Async XLA Ops:
  0.0 0.7 copy-start.3
  0.7 0.7 copy-start.4
  1.3 0.7 copy-start.2
  2.0 1.0 %copy-start = (f32[4,2,128,128]{3,2,1,0:T(8,128)S(1)}, f32[4,2,128,128]{3,2,1,0:T(8,128)}, u32[]{:S(2)}) copy-start(f32[4,2,128,128]{3,2,1,0:T(8,128)} %blocks_hbm.1) | copy-start | bytes 1572868
  3.1 0.7 copy-start.1
